TPU v7x, 32 devices: a whole 2x2x4 slice. The times are simulated.
32 devices in a mesh: member: 4 (over y, x), lat: 2 (over core), lon: 4 (over z).
Axes of the slice: x: 2, y: 2, z: 4, core: 2. Of those that a mesh axis runs over, the one named last changes fastest.
Arguments:
- ice_flux: float32 [8, 64, 8, 512], P(('member', 'lat'), 'lon'), parts along dimension 0, may hold values from 0.5 to 1.5
- ice_frac: float32 [8, 64, 512], P(('member', 'lat'), 'lon'), parts along dimension 0, may hold values from 0.05 to 1
- ice_mask: int32 [8, 64, 512], P(('member', 'lat'), 'lon'), parts along dimension 0, may hold values 0 or 1
- ice_area: float32 [8, 64, 512], P(('member', 'lat'), 'lon'), parts along dimension 0, may hold values from 0.7 to 44.3
- route: int32 [8, 64], P(('member', 'lat'), 'lon'), parts along dimension 0, may hold values from 0 to 63, as said below
- ocean_area: float32 [512, 512], P(('member', 'lat'), 'lon'), parts along dimension 0, may hold values from 0.7 to 44.3
- ocean_wet: int32 [512, 512], P(('member', 'lat'), 'lon'), parts along dimension 0, may hold values 0 or 1
- exponent: int32 [8], replicated, may hold values from 0 to 3
Outputs:
- ocean_flux: float32 [8, 512, 512], P(None, ('member', 'lat'), 'lon'), parts along dimension 1
- source_total: float32 [32], P('member'), parts along dimension 0
There are 4 independent parts, one for each index of `member`. A program takes and returns all parts, laid end to end along the dimension named above; an argument that names none is the same for every part. Nothing has to cross between parts.
Inputs may be any that keep to these rules, and one draw needn't show every extreme that they name: Within each latitude tile row, route is a permutation of 0 to 63. The 16 entries of one device name, for every longitude tile k that they name (route // 16 == k), exactly 4 blocks of it.
All inputs are finite; a program needn't handle non-finite values. No bound on the sum of `ice_mask` or of `ocean_wet` on one device may be relied on, other than what follows from the above.
Results may differ from a plain program's by a relative error of at most 0.0003.
Values sent between devices are 32-bit elements; how exact they have to be, the bound alone decides.
A program may use at most 64 MiB of HBM per device.

v0:
```python
import jax
import jax.numpy as jnp
from jax import lax
from jax.sharding import PartitionSpec as P

quantum = 1024.0
limb_base = 65536


def local_units(values, axes):
    return jnp.sum((values * quantum).astype(jnp.int32), axis=axes)


def split_units(total):
    upper_part = total // limb_base
    return (upper_part, total - upper_part * limb_base)


def join_units(upper_part, lower_part):
    return (upper_part.astype(jnp.float32) * limb_base + lower_part.astype(jnp.float32)) / quantum


def body(ice_flux, ice_frac, ice_mask, ice_area, route, ocean_area, ocean_wet, exponent):
    block_count = route.shape[1]
    field_count = ice_flux.shape[2]
    block_cells = ice_flux.shape[3]
    width_cells = ocean_area.shape[1]
    band_rows = block_cells // width_cells
    tile_count = lax.axis_size("lon")
    amount = ice_area * ice_frac * ice_mask.astype(jnp.float32)
    carried = ice_flux * amount[:, :, None, :]
    source_upper, source_lower = split_units(local_units(carried, (0, 1, 3)))
    block_ids = jnp.arange(block_count, dtype=jnp.int32)
    capacity = max(2, block_count // tile_count)
    targets = route[0]
    target_tile = targets // block_count
    block_row = targets % block_count
    earlier = (target_tile[:, None] == target_tile[None, :]) & (
        block_ids[:, None] > block_ids[None, :]
    )
    ordinal = jnp.sum(earlier.astype(jnp.int32), axis=1)
    slot_index = target_tile * capacity + ordinal
    slot_ids = jnp.arange(tile_count * capacity, dtype=jnp.int32)
    selector = (slot_index[None, :] == slot_ids[:, None]).astype(jnp.float32)
    outgoing = jnp.einsum("qs,sfc->qfc", selector, carried[0], precision=lax.Precision.HIGHEST)
    outgoing_rows = (
        jnp.dot(selector, (block_row + 1).astype(jnp.float32), precision=lax.Precision.HIGHEST)
        - 1.0
    )
    received_rows, arrived_rows = (
        lax.all_to_all(outgoing, "lon", split_axis=0, concat_axis=0, tiled=True),
        lax.all_to_all(outgoing_rows, "lon", split_axis=0, concat_axis=0, tiled=True),
    )
    position_mapper = (arrived_rows[None, :] == block_ids.astype(jnp.float32)[:, None]).astype(
        jnp.float32
    )
    block_groups = jnp.einsum(
        "nw,whl->nhl", position_mapper, received_rows, precision=lax.Precision.HIGHEST
    )
    mapped = block_groups.reshape(block_count, field_count, band_rows, width_cells).transpose(
        1, 0, 2, 3
    )
    mapped = mapped.reshape(field_count, block_count * band_rows, width_cells)
    wet_cover = ocean_wet.astype(jnp.float32)
    target_upper, target_lower = split_units(local_units(wet_cover * mapped, (1, 2)))
    wet_upper, wet_lower = split_units(local_units(ocean_area * wet_cover, (0, 1)))
    source_upper, source_lower, target_upper, target_lower, wet_upper, wet_lower = lax.psum(
        (source_upper, source_lower, target_upper, target_lower, wet_upper, wet_lower),
        ("lat", "lon"),
    )
    source = join_units(source_upper, source_lower)
    target = join_units(target_upper, target_lower)
    wet_area = join_units(wet_upper, wet_lower)
    correction = (source - target) / wet_area
    scaling = jnp.left_shift(jnp.ones_like(exponent), exponent).astype(jnp.float32)
    ocean_flux = (
        wet_cover * scaling[:, None, None] * (mapped / ocean_area + correction[:, None, None])
    )
    return (ocean_flux, source * scaling)


def solution(mesh):
    placed = (
        P(("member", "lat"), "lon", None, None),
        P(("member", "lat"), "lon", None),
        P(("member", "lat"), "lon", None),
        P(("member", "lat"), "lon", None),
        P(("member", "lat"), "lon"),
        P(("member", "lat"), "lon"),
        P(("member", "lat"), "lon"),
        P(),
    )
    return jax.shard_map(
        body,
        mesh=mesh,
        in_specs=placed,
        out_specs=(P(None, ("member", "lat"), "lon"), P("member")),
        check_vma=False,
    )
```

profile of v0, /device:TPU:0, one launch (start us, length us, event | category | flops | bytes accessed | tf_op | source)
XLA Modules:
  0.0 37.0 jit_solution(16438708426224895348)
XLA Ops:
  0.6 0.7 %fusion.29 = s32[16]{0:T(128)S(1)} fusion(s32[1,16]{1,0:T(1,128)} %param.12), kind=kLoop, calls=%fused_computation.62 | loop fusion | flops 240 | bytes 128 | tf_op jit(solution)/shard_map/eq | solution.py:38
  1.4 0.2 convert_reduce_fusion.2
  1.6 0.1 fusion
  1.7 0.7 %all_to_all.9 = f32[4,4,1]{1,0,2:T(4,128)} reshape(f32[16]{0:T(128)S(1)} %fusion) | data formatting | bytes 128 | tf_op jit(solution)/shard_map/all_to_all | solution.py:52
  2.4 6.3 %all-to-all-start = ((f32[4,4,1]{1,2,0:T(1,128)}), f32[4,4,1]{1,2,0:T(1,128)S(1)}, u32[]{:S(2)}, u32[]{:S(2)}) async-start(f32[4,4,1]{1,2,0:T(1,128)} %bitcast.6), calls=%async_computation | async-start | bytes 4096 | tf_op jit(solution)/shard_map/all_to_all | solution.py:52
  8.8 0.8 %multiply_bitcast_fusion.1 = f32[16,512]{1,0:T(8,128)S(1)} fusion(s32[1,16,512]{2,1,0:T(8,128)S(1)} %copy-done.3, f32[1,16,512]{2,1,0:T(8,128)} %param.11, f32[1,16,512]{2,1,0:T(8,128)} %param.9), kind=kLoop, calls=%fused_computation.14 | loop fusion | flops 24576 | bytes 131072 | tf_op jit(solution)/shard_map/mul | solution.py:31
  9.5 1.0 %multiply_bitcast_fusion = f32[16,8,512]{2,1,0:T(8,128)S(1)} fusion(f32[1,16,8,512]{3,2,1,0:T(8,128)} %param.8, f32[16,512]{1,0:T(8,128)S(1)} %multiply_bitcast_fusion.1), kind=kLoop, calls=%fused_computation.12 | loop fusion | flops 65536 | bytes 557056 | tf_op jit(solution)/shard_map/squeeze | solution.py:45
  10.6 0.4 %fusion.6 = f32[16,8,512]{2,0,1:T(8,128)S(1)} fusion(f32[16,8,512]{2,1,0:T(8,128)S(1)} %multiply_bitcast_fusion, s32[16]{0:T(128)S(1)} %fusion.21), kind=kOutput, calls=%fused_computation.8 | convolution fusion | flops 12583168 | bytes 524352 | tf_op jit(solution)/shard_map/qs,sfc->qfc/dot_general | solution.py:45
  11.0 0.2 copy-done.4
  11.2 0.1 copy-done.1
  11.3 0.6 %convert_reduce_fusion.1 = (s32[]{:T(128)}, f32[64,128]{1,0:T(8,128)S(1)}) fusion(f32[64,128]{1,0:T(8,128)S(1)} %copy-done.1, s32[64,128]{1,0:T(8,128)S(1)} %copy-done.2), kind=kLoop, calls=%fused_computation.13 | loop fusion | flops 40959 | bytes 98308 | tf_op jit(solution)/shard_map/reduce_sum | solution.py:11
  12.0 0.9 %copy.14 = f32[16,8,512]{2,1,0:T(8,128)} copy(f32[16,8,512]{2,0,1:T(8,128)S(1)} %fusion.6) | data formatting | bytes 524288 | tf_op jit(solution)/shard_map/qs,sfc->qfc/dot_general | solution.py:45
  12.8 1.4 %all-to-all-done = f32[4,4,1]{1,2,0:T(1,128)S(1)} async-done(((f32[4,4,1]{1,2,0:T(1,128)}), f32[4,4,1]{1,2,0:T(1,128)S(1)}, u32[]{:S(2)}, u32[]{:S(2)}) %all-to-all-start) | async-done | bytes 96 | tf_op jit(solution)/shard_map/all_to_all | solution.py:52
  14.2 3.9 %all-to-all-start.1 = ((f32[16,8,512]{2,1,0:T(8,128)}), f32[16,8,512]{2,1,0:T(8,128)S(1)}, u32[]{:S(2)}, u32[]{:S(2)}) async-start(f32[16,8,512]{2,1,0:T(8,128)} %copy.14), calls=%async_computation.1 | async-start | bytes 524288 | tf_op jit(solution)/shard_map/all_to_all | solution.py:51
  21.3 0.2 convert_reduce_fusion
  21.5 0.5 %broadcast.161 = f32[]{:T(128)} broadcast(f32[]{:T(128)} %constant.126), dimensions={} | broadcast | bytes 8 | tf_op jit(solution)/shard_map/all_to_all | solution.py:52
  22.0 0.7 %reduce.4 = f32[4,4]{1,0:T(4,128)S(1)} reduce(f32[4,4,1]{1,2,0:T(1,128)S(1)} %all-to-all-done, f32[]{:T(128)} %broadcast.161), dimensions={2}, to_apply=%all_to_all.10.reduce_sub_computation.3 | reduce | bytes 132 | tf_op jit(solution)/shard_map/all_to_all | solution.py:52
  22.8 3.6 %all-to-all-done.1 = f32[16,8,512]{2,1,0:T(8,128)S(1)} async-done(((f32[16,8,512]{2,1,0:T(8,128)}), f32[16,8,512]{2,1,0:T(8,128)S(1)}, u32[]{:S(2)}, u32[]{:S(2)}) %all-to-all-start.1) | async-done | bytes 262176 | tf_op jit(solution)/shard_map/all_to_all | solution.py:51
  26.4 0.4 %fusion.4 = f32[16,8,512]{2,0,1:T(8,128)S(1)} fusion(f32[16,8,512]{2,1,0:T(8,128)S(1)} %all-to-all-done.1, f32[16]{0:T(128)S(1)} %eq.52, f32[16]{0:T(128)S(1)} %iota_convert_fusion), kind=kOutput, calls=%fused_computation.6 | convolution fusion | flops 12583168 | bytes 524416 | tf_op jit(solution)/shard_map/nw,whl->nhl/dot_general | solution.py:57
  26.8 0.1 reshape.55
  26.9 0.3 fusion.3
  27.2 7.2 %all-reduce = (s32[8]{0:T(128)S(1)}, s32[8]{0:T(128)S(1)}, s32[]{:T(128)}, s32[]{:T(128)}, s32[8]{0:T(128)S(1)}, /*index=5*/s32[8]{0:T(128)S(1)}) all-reduce(s32[8]{0:T(128)S(1)} %get-tuple-element.10, s32[8]{0:T(128)S(1)} %get-tuple-element.11, s32[]{:T(128)S(6)} %select_n.37, ...), channel_id=1, replica_groups=mesh['member'=4,'lat'=2,'lon'=4] {'lat','lon'}, use_global_device_ids=true, to_apply=%region_6.7 | all-reduce | flops 34 | bytes 272 | tf_op jit(solution)/shard_map/psum | solution.py:67
  35.7 0.5 %fusion.28 = (f32[8]{0:T(128)}, f32[8]{0:T(128)S(1)}) fusion(s32[8]{0:T(128)S(1)} %copy-done.4, s32[8]{0:T(128)S(1)} %get-tuple-element.6, s32[8]{0:T(128)S(1)} %get-tuple-element.7, f32[]{:T(128)S(6)} %div.93, s32[8]{0:T(128)S(1)} %get-tuple-element.2, s32[8]{0:T(128)S(1)} %get-tuple-element.3), kind=kLoop, calls=%fused_computation.61 | loop fusion | flops 120 | bytes 228 | tf_op jit(solution)/shard_map/mul | solution.py:79
  36.2 0.8 %add_multiply_fusion = f32[8,64,128]{2,1,0:T(8,128)} fusion(f32[8,64,128]{2,1,0:T(8,128)S(1)} %bitcast.56, f32[8]{0:T(128)S(1)} %get-tuple-element.15, f32[64,128]{1,0:T(8,128)S(1)} %copy-done.1, f32[8]{0:T(128)S(1)} %shift-left_convert_fusion, f32[64,128]{1,0:T(8,128)S(1)} %get-tuple-element.13), kind=kLoop, calls=%fused_computation.10 | loop fusion | flops 262144 | bytes 589888 | tf_op jit(solution)/shard_map/mul | solution.py:77
  (17 shorter events, 0.2 us)
Async XLA Ops:
  0.6 0.7 %copy-start.5 = (s32[1,16]{1,0:T(1,128)S(1)}, s32[1,16]{1,0:T(1,128)}, u32[]{:S(2)}) copy-start(s32[1,16]{1,0:T(1,128)} %param.12) | copy-start | bytes 196
  0.6 8.1 %copy-start.3 = (s32[1,16,512]{2,1,0:T(8,128)S(1)}, s32[1,16,512]{2,1,0:T(8,128)}, u32[]{:S(2)}) copy-start(s32[1,16,512]{2,1,0:T(8,128)} %param.10) | copy-start | bytes 98308
  2.4 11.8 %all-to-all-start = ((f32[4,4,1]{1,2,0:T(1,128)}), f32[4,4,1]{1,2,0:T(1,128)S(1)}, u32[]{:S(2)}, u32[]{:S(2)}) async-start(f32[4,4,1]{1,2,0:T(1,128)} %bitcast.6), calls=%async_computation | async-start | bytes 4096 | tf_op jit(solution)/shard_map/all_to_all | solution.py:52
  10.5 0.7 %copy-start.4 = (s32[8]{0:T(128)S(1)}, s32[8]{0:T(128)}, u32[]{:S(2)}) copy-start(s32[8]{0:T(128)} %param.15) | copy-start | bytes 100
  10.5 0.8 %copy-start.1 = (f32[64,128]{1,0:T(8,128)S(1)}, f32[64,128]{1,0:T(8,128)}, u32[]{:S(2)}) copy-start(f32[64,128]{1,0:T(8,128)} %param.13) | copy-start | bytes 98308
  10.6 0.8 %copy-start.2 = (s32[64,128]{1,0:T(8,128)S(1)}, s32[64,128]{1,0:T(8,128)}, u32[]{:S(2)}) copy-start(s32[64,128]{1,0:T(8,128)} %param.14) | copy-start | bytes 98308
  12.8 8.5 %copy-start = (f32[1,16,8,512]{3,2,1,0:T(8,128)S(1)}, f32[1,16,8,512]{3,2,1,0:T(8,128)}, u32[]{:S(2)}) copy-start(f32[1,16,8,512]{3,2,1,0:T(8,128)} %param.8) | copy-start | bytes 786436
  14.2 12.2 %all-to-all-start.1 = ((f32[16,8,512]{2,1,0:T(8,128)}), f32[16,8,512]{2,1,0:T(8,128)S(1)}, u32[]{:S(2)}, u32[]{:S(2)}) async-start(f32[16,8,512]{2,1,0:T(8,128)} %copy.14), calls=%async_computation.1 | async-start | bytes 524288 | tf_op jit(solution)/shard_map/all_to_all | solution.py:51
where the time goes:
time: 37.6 us; the launch traced here: 37 us
  starting transfers between devices  10.2 us (27%)
  blocking collectives  7.23 us (19%)
  other arithmetic  5.81 us (15%)
  between operations  5.28 us (14%)
  waiting for transfers between devices  4.93 us (13%)
  local copies, waits for them, and re-layouts  2.61 us (7%)
  matrix products  0.94 us (2%)
    psum x1, blocking collectives, body(): lax.psum((source_upper, source_lower, target_upper, target_lower, wet_upp...  7.23 us
    all_to_all x1, starting transfers between devices, body(): lax.all_to_all(outgoing_rows, 'lon', split_axis=0, concat_axis=0, tiled=T...  6.35 us
    all_to_all x1, starting transfers between devices, body(): lax.all_to_all(outgoing, 'lon', split_axis=0, concat_axis=0, tiled=True)  3.88 us
    all_to_all x1, waiting for transfers between devices, body(): lax.all_to_all(outgoing, 'lon', split_axis=0, concat_axis=0, tiled=True)  3.58 us
    all_to_all x1, waiting for transfers between devices, body(): lax.all_to_all(outgoing_rows, 'lon', split_axis=0, concat_axis=0, tiled=T...  1.35 us
    all_to_all x2, local copies, waits for them, and re-layouts, body(): lax.all_to_all(outgoing_rows, 'lon', split_axis=0, concat_axis=0, tiled=T...  1.21 us
    reduce_sum x3, other arithmetic, local_units(): return jnp.sum((values * quantum).astype(jnp.int32), axis=axes)  1.1 us
    squeeze x1, other arithmetic, body(): carried[0]  0.98 us
  transfers between devices with their start and end apart: 2, of which 2 were waited for; matrix products, arithmetic and copies ran while one was open for 14% of the time, Pallas kernels for 0%

commit v1 on v0

--- a/solution.py
+++ b/solution.py
@@ -5,6 +5,11 @@
 
 quantum = 1024.0
 limb_base = 65536
+
+
+def one_after_other(array, inner_axis, outer_axis):
+    inner = lax.psum(array, inner_axis)
+    return lax.psum(inner, outer_axis)
 
 
 def local_units(values, axes):
@@ -64,9 +69,8 @@
     wet_cover = ocean_wet.astype(jnp.float32)
     target_upper, target_lower = split_units(local_units(wet_cover * mapped, (1, 2)))
     wet_upper, wet_lower = split_units(local_units(ocean_area * wet_cover, (0, 1)))
-    source_upper, source_lower, target_upper, target_lower, wet_upper, wet_lower = lax.psum(
-        (source_upper, source_lower, target_upper, target_lower, wet_upper, wet_lower),
-        ("lat", "lon"),
+    source_upper, source_lower, target_upper, target_lower, wet_upper, wet_lower = one_after_other(
+        (source_upper, source_lower, target_upper, target_lower, wet_upper, wet_lower), "lon", "lat"
     )
     source = join_units(source_upper, source_lower)
     target = join_units(target_upper, target_lower)

time: 37.6 us -> 39.2 us (1.043)
  blocking collectives: 7.23 us -> 8.87 us
    psum x1 -> x2, blocking collectives: 7.23 us -> 8.87 us  [the longest x1 6.42 us: one_after_other(): inner = lax.psum(array, inner_axis)]
  transfers between devices with their start and end apart: 2 -> 2, of which waited for: 2 -> 2; matrix products, arithmetic and copies ran while one was open for 14% -> 13% of each run, Pallas kernels for 0% -> 0%
where the time goes in v1:
time: 39.2 us; the launch traced here: 38.7 us
  starting transfers between devices  10.2 us (26%)
  blocking collectives  8.87 us (23%)
  other arithmetic  5.81 us (15%)
  between operations  5.28 us (13%)
  waiting for transfers between devices  4.93 us (13%)
  local copies, waits for them, and re-layouts  2.61 us (7%)
  matrix products  0.94 us (2%)
    psum x1, blocking collectives, one_after_other(): inner = lax.psum(array, inner_axis)  6.42 us
    all_to_all x1, starting transfers between devices, body(): lax.all_to_all(outgoing_rows, 'lon', split_axis=0, concat_axis=0, tiled=T...  6.35 us
    all_to_all x1, starting transfers between devices, body(): lax.all_to_all(outgoing, 'lon', split_axis=0, concat_axis=0, tiled=True)  3.88 us
    all_to_all x1, waiting for transfers between devices, body(): lax.all_to_all(outgoing, 'lon', split_axis=0, concat_axis=0, tiled=True)  3.58 us
    psum x1, blocking collectives, one_after_other(): return lax.psum(inner, outer_axis)  2.46 us
    all_to_all x1, waiting for transfers between devices, body(): lax.all_to_all(outgoing_rows, 'lon', split_axis=0, concat_axis=0, tiled=T...  1.35 us
    all_to_all x2, local copies, waits for them, and re-layouts, body(): lax.all_to_all(outgoing_rows, 'lon', split_axis=0, concat_axis=0, tiled=T...  1.21 us
    reduce_sum x3, other arithmetic, local_units(): return jnp.sum((values * quantum).astype(jnp.int32), axis=axes)  1.1 us
  transfers between devices with their start and end apart: 2, of which 2 were waited for; matrix products, arithmetic and copies ran while one was open for 13% of the time, Pallas kernels for 0%

profile of v1, /device:TPU:0, one launch (start us, length us, event | category | flops | bytes accessed | tf_op | source)
XLA Modules:
  0.0 38.7 jit_solution(15088510409496898125)
XLA Ops:
  0.6 0.7 %fusion.29 = s32[16]{0:T(128)S(1)} fusion(s32[1,16]{1,0:T(1,128)} %param.12), kind=kLoop, calls=%fused_computation.62 | loop fusion | flops 240 | bytes 128 | tf_op jit(solution)/shard_map/eq | solution.py:43
  1.4 0.2 convert_reduce_fusion.2
  1.6 0.1 fusion
  1.7 0.7 %all_to_all.9 = f32[4,4,1]{1,0,2:T(4,128)} reshape(f32[16]{0:T(128)S(1)} %fusion) | data formatting | bytes 128 | tf_op jit(solution)/shard_map/all_to_all | solution.py:57
  2.4 6.3 %all-to-all-start = ((f32[4,4,1]{1,2,0:T(1,128)}), f32[4,4,1]{1,2,0:T(1,128)S(1)}, u32[]{:S(2)}, u32[]{:S(2)}) async-start(f32[4,4,1]{1,2,0:T(1,128)} %bitcast.6), calls=%async_computation | async-start | bytes 4096 | tf_op jit(solution)/shard_map/all_to_all | solution.py:57
  8.8 0.8 %multiply_bitcast_fusion.1 = f32[16,512]{1,0:T(8,128)S(1)} fusion(s32[1,16,512]{2,1,0:T(8,128)S(1)} %copy-done.3, f32[1,16,512]{2,1,0:T(8,128)} %param.11, f32[1,16,512]{2,1,0:T(8,128)} %param.9), kind=kLoop, calls=%fused_computation.14 | loop fusion | flops 24576 | bytes 131072 | tf_op jit(solution)/shard_map/mul | solution.py:36
  9.5 1.0 %multiply_bitcast_fusion = f32[16,8,512]{2,1,0:T(8,128)S(1)} fusion(f32[1,16,8,512]{3,2,1,0:T(8,128)} %param.8, f32[16,512]{1,0:T(8,128)S(1)} %multiply_bitcast_fusion.1), kind=kLoop, calls=%fused_computation.12 | loop fusion | flops 65536 | bytes 557056 | tf_op jit(solution)/shard_map/squeeze | solution.py:50
  10.6 0.4 %fusion.6 = f32[16,8,512]{2,0,1:T(8,128)S(1)} fusion(f32[16,8,512]{2,1,0:T(8,128)S(1)} %multiply_bitcast_fusion, s32[16]{0:T(128)S(1)} %fusion.21), kind=kOutput, calls=%fused_computation.8 | convolution fusion | flops 12583168 | bytes 524352 | tf_op jit(solution)/shard_map/qs,sfc->qfc/dot_general | solution.py:50
  11.0 0.2 copy-done.4
  11.2 0.1 copy-done.1
  11.3 0.6 %convert_reduce_fusion.1 = (s32[]{:T(128)}, f32[64,128]{1,0:T(8,128)S(1)}) fusion(f32[64,128]{1,0:T(8,128)S(1)} %copy-done.1, s32[64,128]{1,0:T(8,128)S(1)} %copy-done.2), kind=kLoop, calls=%fused_computation.13 | loop fusion | flops 40959 | bytes 98308 | tf_op jit(solution)/shard_map/reduce_sum | solution.py:16
  12.0 0.9 %copy.14 = f32[16,8,512]{2,1,0:T(8,128)} copy(f32[16,8,512]{2,0,1:T(8,128)S(1)} %fusion.6) | data formatting | bytes 524288 | tf_op jit(solution)/shard_map/qs,sfc->qfc/dot_general | solution.py:50
  12.8 1.4 %all-to-all-done = f32[4,4,1]{1,2,0:T(1,128)S(1)} async-done(((f32[4,4,1]{1,2,0:T(1,128)}), f32[4,4,1]{1,2,0:T(1,128)S(1)}, u32[]{:S(2)}, u32[]{:S(2)}) %all-to-all-start) | async-done | bytes 96 | tf_op jit(solution)/shard_map/all_to_all | solution.py:57
  14.2 3.9 %all-to-all-start.1 = ((f32[16,8,512]{2,1,0:T(8,128)}), f32[16,8,512]{2,1,0:T(8,128)S(1)}, u32[]{:S(2)}, u32[]{:S(2)}) async-start(f32[16,8,512]{2,1,0:T(8,128)} %copy.14), calls=%async_computation.1 | async-start | bytes 524288 | tf_op jit(solution)/shard_map/all_to_all | solution.py:56
  21.3 0.2 convert_reduce_fusion
  21.5 0.5 %broadcast.161 = f32[]{:T(128)} broadcast(f32[]{:T(128)} %constant.126), dimensions={} | broadcast | bytes 8 | tf_op jit(solution)/shard_map/all_to_all | solution.py:57
  22.0 0.7 %reduce.4 = f32[4,4]{1,0:T(4,128)S(1)} reduce(f32[4,4,1]{1,2,0:T(1,128)S(1)} %all-to-all-done, f32[]{:T(128)} %broadcast.161), dimensions={2}, to_apply=%all_to_all.10.reduce_sub_computation.3 | reduce | bytes 132 | tf_op jit(solution)/shard_map/all_to_all | solution.py:57
  22.8 3.6 %all-to-all-done.1 = f32[16,8,512]{2,1,0:T(8,128)S(1)} async-done(((f32[16,8,512]{2,1,0:T(8,128)}), f32[16,8,512]{2,1,0:T(8,128)S(1)}, u32[]{:S(2)}, u32[]{:S(2)}) %all-to-all-start.1) | async-done | bytes 262176 | tf_op jit(solution)/shard_map/all_to_all | solution.py:56
  26.4 0.4 %fusion.4 = f32[16,8,512]{2,0,1:T(8,128)S(1)} fusion(f32[16,8,512]{2,1,0:T(8,128)S(1)} %all-to-all-done.1, f32[16]{0:T(128)S(1)} %eq.52, f32[16]{0:T(128)S(1)} %iota_convert_fusion), kind=kOutput, calls=%fused_computation.6 | convolution fusion | flops 12583168 | bytes 524416 | tf_op jit(solution)/shard_map/nw,whl->nhl/dot_general | solution.py:62
  26.9 0.3 fusion.3
  27.2 6.4 %all-reduce = (s32[8]{0:T(128)S(1)}, s32[8]{0:T(128)S(1)}, s32[]{:T(128)}, s32[]{:T(128)}, s32[8]{0:T(128)S(1)}, /*index=5*/s32[8]{0:T(128)S(1)}) all-reduce(s32[8]{0:T(128)S(1)} %get-tuple-element.16, s32[8]{0:T(128)S(1)} %get-tuple-element.17, s32[]{:T(128)S(6)} %select_n.37, ...), channel_id=1, replica_groups=mesh['member'=4,'lat'=2,'lon'=4] {'lon'}, use_global_device_ids=true, to_apply=%region_9.10 | all-reduce | flops 34 | bytes 272 | tf_op jit(solution)/shard_map/psum | solution.py:11
  33.6 2.5 %all-reduce.1 = (s32[8]{0:T(128)S(1)}, s32[8]{0:T(128)S(1)}, s32[]{:T(128)}, s32[]{:T(128)}, s32[8]{0:T(128)S(1)}, /*index=5*/s32[8]{0:T(128)S(1)}) all-reduce(s32[8]{0:T(128)S(1)} %get-tuple-element.2, s32[8]{0:T(128)S(1)} %get-tuple-element.3, s32[]{:T(128)} %get-tuple-element.4, ...), channel_id=1, replica_groups=mesh['member'=4,'lat'=2,'lon'=4] {'lat'}, use_global_device_ids=true, to_apply=%region_10.11 | all-reduce | flops 34 | bytes 272 | tf_op jit(solution)/shard_map/psum | solution.py:12
  37.3 0.5 %fusion.28 = (f32[8]{0:T(128)}, f32[8]{0:T(128)S(1)}) fusion(s32[8]{0:T(128)S(1)} %copy-done.4, s32[8]{0:T(128)S(1)} %get-tuple-element.12, s32[8]{0:T(128)S(1)} %get-tuple-element.13, f32[]{:T(128)S(6)} %div.93, s32[8]{0:T(128)S(1)} %get-tuple-element.8, s32[8]{0:T(128)S(1)} %get-tuple-element.9), kind=kLoop, calls=%fused_computation.61 | loop fusion | flops 120 | bytes 228 | tf_op jit(solution)/shard_map/mul | solution.py:83
  37.9 0.8 %add_multiply_fusion = f32[8,64,128]{2,1,0:T(8,128)} fusion(f32[8,64,128]{2,1,0:T(8,128)S(1)} %bitcast.56, f32[8]{0:T(128)S(1)} %get-tuple-element.21, f32[64,128]{1,0:T(8,128)S(1)} %copy-done.1, f32[8]{0:T(128)S(1)} %shift-left_convert_fusion, f32[64,128]{1,0:T(8,128)S(1)} %get-tuple-element.19), kind=kLoop, calls=%fused_computation.10 | loop fusion | flops 262144 | bytes 589888 | tf_op jit(solution)/shard_map/mul | solution.py:81
  (18 shorter events, 0.3 us)
Async XLA Ops:
  0.6 0.7 %copy-start.5 = (s32[1,16]{1,0:T(1,128)S(1)}, s32[1,16]{1,0:T(1,128)}, u32[]{:S(2)}) copy-start(s32[1,16]{1,0:T(1,128)} %param.12) | copy-start | bytes 196
  0.6 8.1 %copy-start.3 = (s32[1,16,512]{2,1,0:T(8,128)S(1)}, s32[1,16,512]{2,1,0:T(8,128)}, u32[]{:S(2)}) copy-start(s32[1,16,512]{2,1,0:T(8,128)} %param.10) | copy-start | bytes 98308
  2.4 11.8 %all-to-all-start = ((f32[4,4,1]{1,2,0:T(1,128)}), f32[4,4,1]{1,2,0:T(1,128)S(1)}, u32[]{:S(2)}, u32[]{:S(2)}) async-start(f32[4,4,1]{1,2,0:T(1,128)} %bitcast.6), calls=%async_computation | async-start | bytes 4096 | tf_op jit(solution)/shard_map/all_to_all | solution.py:57
  10.5 0.7 %copy-start.4 = (s32[8]{0:T(128)S(1)}, s32[8]{0:T(128)}, u32[]{:S(2)}) copy-start(s32[8]{0:T(128)} %param.15) | copy-start | bytes 100
  10.5 0.8 %copy-start.1 = (f32[64,128]{1,0:T(8,128)S(1)}, f32[64,128]{1,0:T(8,128)}, u32[]{:S(2)}) copy-start(f32[64,128]{1,0:T(8,128)} %param.13) | copy-start | bytes 98308
  10.6 0.8 %copy-start.2 = (s32[64,128]{1,0:T(8,128)S(1)}, s32[64,128]{1,0:T(8,128)}, u32[]{:S(2)}) copy-start(s32[64,128]{1,0:T(8,128)} %param.14) | copy-start | bytes 98308
  12.8 8.5 %copy-start = (f32[1,16,8,512]{3,2,1,0:T(8,128)S(1)}, f32[1,16,8,512]{3,2,1,0:T(8,128)}, u32[]{:S(2)}) copy-start(f32[1,16,8,512]{3,2,1,0:T(8,128)} %param.8) | copy-start | bytes 786436
  14.2 12.2 %all-to-all-start.1 = ((f32[16,8,512]{2,1,0:T(8,128)}), f32[16,8,512]{2,1,0:T(8,128)S(1)}, u32[]{:S(2)}, u32[]{:S(2)}) async-start(f32[16,8,512]{2,1,0:T(8,128)} %copy.14), calls=%async_computation.1 | async-start | bytes 524288 | tf_op jit(solution)/shard_map/all_to_all | solution.py:56
